TPU v7x, 128 devices: a whole 4x4x4 slice. The times are simulated.
128 devices in a mesh: col: 32 (over y, z, core), grp: 4 (over x).
Axes of the slice: x: 4, y: 4, z: 4, core: 2. Of those that a mesh axis runs over, the one named last changes fastest.
Arguments:
- density_now: float32 [2, 32768, 768], P(None, ('col', 'grp')), may hold values from -6 to 6
- density_before: float32 [2, 32768, 768], P(None, ('col', 'grp')), may hold values from -6 to 6
- source: float32 [2, 32768, 768], P(None, ('col', 'grp')), may hold values from -8 to 8
- response: float32 [32768, 768], P(('col', 'grp')), may hold values from 0.5 to 4
- history_density: bfloat16 [7, 2, 32768, 768], P(None, None, ('col', 'grp')), may hold values from -6 to 6
- history_residual: bfloat16 [7, 2, 32768, 768], P(None, None, ('col', 'grp')), may hold values from -6 to 6
- column_shell: int32 [32768], P(('col', 'grp')), may hold values from 1 to 131072, as said below
- screening: float32 [1], replicated, may hold values from 1466 to 36672
Outputs:
- slab_density: float32 [2, 2, 768, 32768], P(None, None, 'col', 'grp')
- mixed_density: float32 [2, 32768, 768], P(None, ('col', 'grp'))
- residual_norm: float32 [2], replicated
Inputs may be any that keep to these rules, and one draw needn't show every extreme that they name: `column_shell`: column j's value lies between 1 + j * s and (j + 1) * s, where s = (383^2 - 1) // 32768.
All inputs are finite; a program needn't handle non-finite values.
Results may differ from a plain program's by a relative error of at most 0.0038.
Values sent between devices are 32-bit elements; how exact they have to be, the bound alone decides.
A program may use at most 192 MiB of HBM per device.

v0:
```python
import math

import jax
import jax.numpy as jnp
from jax import lax
from jax.sharding import Mesh
from jax.sharding import PartitionSpec as P

HIST = 8
ITERS = 2
COL_GRP = ("col_0", "col_1", "col_2", "grp")
COL = ("col_0", "col_1", "col_2")


MIXING = 0.7


def by_axis(array, axes):
    for axis in axes:
        array = lax.psum(array, axis)
    return array


def geometry(column_shell, screening, plane_count):
    midpoint = plane_count // 2
    slot_index = jnp.arange(plane_count, dtype=jnp.int32)
    signed = jnp.where(slot_index < midpoint, slot_index, slot_index - plane_count)
    squared = column_shell[:, None] + signed[None, :] * signed[None, :]
    inside = squared <= (midpoint - 1) * (midpoint - 1)
    shells = squared.astype(jnp.float32)
    screen = screening[0]
    precond = MIXING * shells / (shells + screen)
    metric = jnp.where(inside, (shells + screen) / shells, jnp.float32(0.0))
    return (inside.astype(jnp.float32), precond, metric)


def plane_table(plane_count):
    slot_index = jnp.arange(plane_count, dtype=jnp.int32)
    phase = slot_index[:, None] * slot_index[None, :] % plane_count
    angle = phase.astype(jnp.float32) * jnp.float32(2.0 * math.pi / plane_count)
    spread = jnp.float32(1.0 / math.sqrt(plane_count))
    return jnp.concatenate([jnp.cos(angle), jnp.sin(angle)], axis=0) * spread


def to_planes(dft_table, density):
    components, columns, plane_count = density.shape
    stacked_rows = density.reshape(components * columns, plane_count)
    products = lax.dot_general(
        dft_table,
        stacked_rows,
        (((1,), (1,)), ((), ())),
        precision=lax.Precision.HIGHEST,
        preferred_element_type=jnp.float32,
    )
    cosine = products[:plane_count]
    sine = products[plane_count:]
    real_part = cosine[:, :columns] - sine[:, columns:]
    imag_part = sine[:, :columns] + cosine[:, columns:]
    return jnp.stack([real_part, imag_part])


def flatten_rows(stack):
    return stack.reshape(stack.shape[0], -1)


def inner_rows(first_stack, second_stack):
    return lax.dot_general(
        flatten_rows(first_stack),
        flatten_rows(second_stack),
        (((1,), (1,)), ((), ())),
        preferred_element_type=jnp.float32,
    )


def apply_metric(metric, stack):
    return (metric[None, None] * stack.astype(jnp.float32)).astype(jnp.bfloat16)


def combine_history(coefficients, stack):
    return jnp.sum(coefficients[:, None, None, None] * stack.astype(jnp.float32), axis=0)


def pulay_weights(margin, projections):
    symmetric = 0.5 * (margin + margin.T)
    factor = jnp.linalg.cholesky(symmetric)
    return jax.scipy.linalg.cho_solve((factor, True), projections)


def body(
    density_now,
    density_before,
    source,
    response,
    history_density,
    history_residual,
    column_shell,
    screening,
):
    plane_count = density_now.shape[-1]
    inside_mask, precond, metric = geometry(column_shell, screening, plane_count)
    dft_table = plane_table(plane_count)
    prev_residual = source - response[None] * density_before
    rho_stack = history_density
    res_stack = history_residual
    density = density_now
    previous = density_before
    weighted_stack = apply_metric(metric, history_residual)
    margin, weight_total = (
        by_axis(inner_rows(weighted_stack, history_residual), COL_GRP),
        by_axis(jnp.sum(metric), COL_GRP),
    )
    planes = []
    norms = []
    for iteration in range(ITERS):
        residual = source - response[None] * density
        rho_new = (density - previous).astype(jnp.bfloat16)[None]
        res_new = (residual - prev_residual).astype(jnp.bfloat16)[None]
        dropped = 1 if rho_stack.shape[0] >= HIST else 0
        rho_stack = jnp.concatenate([rho_stack[dropped:], rho_new])
        res_stack = jnp.concatenate([res_stack[dropped:], res_new])
        residual_half = residual.astype(jnp.bfloat16)[None]
        square_local = jnp.sum(metric[None] * residual * residual)
        weighted_new = apply_metric(metric, res_new)
        weighted_stack = jnp.concatenate([weighted_stack[dropped:], weighted_new])
        newest_row = inner_rows(weighted_new, res_stack)[0]
        projection_local = inner_rows(weighted_stack, residual_half)[:, 0]
        newest_row, projections, square = (
            by_axis(newest_row, COL_GRP),
            by_axis(projection_local, COL_GRP),
            by_axis(square_local, COL_GRP),
        )
        old_block = margin[dropped:, dropped:]
        upper = jnp.concatenate([old_block, newest_row[:-1, None]], axis=1)
        margin = jnp.concatenate([upper, newest_row[None]], axis=0)
        coefficients = pulay_weights(margin, projections)
        norms.append(jnp.sqrt(square / weight_total))
        rho_mix = density - combine_history(coefficients, rho_stack)
        res_mix = residual - combine_history(coefficients, res_stack)
        new_density = inside_mask[None] * (rho_mix + precond[None] * res_mix)
        slabs = to_planes(dft_table, new_density)
        planes.append(lax.all_to_all(slabs, COL, split_axis=1, concat_axis=2, tiled=True))
        previous = density
        prev_residual = residual
        density = new_density
    slab_out = jnp.stack(planes)
    return (slab_out, density, jnp.stack(norms))


def solution(mesh):
    finer = Mesh(
        mesh.devices.reshape(4, 4, 2, mesh.shape["grp"]), ("col_0", "col_1", "col_2", "grp")
    )
    return jax.shard_map(
        body,
        mesh=finer,
        in_specs=(
            P(None, COL_GRP, None),
            P(None, COL_GRP, None),
            P(None, COL_GRP, None),
            P(COL_GRP, None),
            P(None, None, COL_GRP, None),
            P(None, None, COL_GRP, None),
            P(COL_GRP),
            P(),
        ),
        out_specs=(P(None, None, COL, "grp"), P(None, COL_GRP, None), P()),
        check_vma=False,
    )
```

profile of v0, /device:TPU:1, one launch (start us, length us, event | category | flops | bytes accessed | tf_op | source)
XLA Modules:
  0.0 280.2 jit_solution(16133113071766164656)
XLA Ops:
  1.4 2.6 fusion.60
  4.0 3.1 %fusion.81 = (bf16[2,256,768]{2,1,0:T(8,128)(2,1)}, f32[2,256,768]{2,1,0:T(8,128)S(1)}) fusion(f32[2,256,768]{2,1,0:T(8,128)} %param.13, f32[2,256,768]{2,1,0:T(8,128)S(1)} %copy-done.1, f32[256,768]{1,0:T(8,128)} %param.14), kind=kLoop, calls=%fused_computation.130 | loop fusion | flops 1179648 | bytes 6291456 | tf_op jit(solution)/shard_map/convert_element_type | solution.py:121
  8.2 2.0 multiply_convert_fusion.2
  10.2 1.4 reshape.199
  11.6 1.4 concatenate.66
  14.1 2.7 concatenate.61
  16.8 4.1 %multiply_convert_fusion = bf16[7,2,256,768]{3,2,1,0:T(8,128)(2,1)S(1)} fusion(bf16[7,2,256,768]{3,2,1,0:T(8,128)(2,1)} %param.16, f32[256,768]{1,0:T(8,128)} %copy-done.11), kind=kLoop, calls=%fused_computation.4 | loop fusion | flops 8257536 | bytes 11796480 | tf_op jit(solution)/shard_map/convert_element_type | solution.py:76
  21.0 5.7 %copy.40 = bf16[1,7,512,768]{3,1,2,0:T(8,128)(2,1)} copy(bf16[1,7,512,768]{3,2,1,0:T(8,128)(2,1)S(1)} %bitcast.119) | data formatting | bytes 11010048
  26.7 9.4 %fusion.35 = f32[7,7]{1,0:T(8,128)S(1)} fusion(bf16[7,2,256,768]{3,2,1,0:T(8,128)(2,1)S(1)} %bitcast.118, bf16[7,2,256,768]{3,2,1,0:T(8,128)(2,1)S(1)} %multiply_convert_fusion), kind=kOutput, calls=%fused_computation.69 | convolution fusion | flops 38535168 | bytes 11010244 | tf_op jit(solution)/shard_map/dot_general | solution.py:67
  36.1 5.9 %copy.41 = bf16[1,7,512,768]{3,1,2,0:T(8,128)(2,1)} copy(bf16[1,7,512,768]{3,2,1,0:T(8,128)(2,1)S(1)} %bitcast.120) | data formatting | bytes 11010048
  42.0 1.4 reshape.201
  43.4 8.8 %fusion.49 = f32[8]{0:T(128)S(1)} fusion(bf16[393216,1]{0,1:T(2,128)(2,1)} %reshape.199, bf16[1,393216]{1,0:T(2,128)(2,1)} %concatenate.61, bf16[7,393216]{1,0:T(8,128)(2,1)} %bitcast.132), kind=kOutput, calls=%fused_computation.73 | convolution fusion | flops 18874368 | bytes 7077920 | tf_op jit(solution)/shard_map/dot_general | solution.py:67
  52.3 4.5 %fusion.46 = f32[8]{0:T(128)S(1)} fusion(bf16[393216,1]{0,1:T(2,128)(2,1)S(1)} %copy-done.38, bf16[1,393216]{1,0:T(2,128)(2,1)S(1)} %copy-done.36, bf16[7,393216]{1,0:T(8,128)(2,1)S(1)} %bitcast.131), kind=kOutput, calls=%fused_computation.72 | convolution fusion | flops 18874368 | bytes 7077920 | tf_op jit(solution)/shard_map/dot_general | solution.py:67
  56.8 10.6 %fusion.29 = (f32[768,768]{1,0:T(8,128)}, f32[768,768]{1,0:T(8,128)}) fusion(), kind=kLoop, calls=%fused_computation.47 | loop fusion | flops 5308416 | bytes 4718592 | tf_op jit(solution)/shard_map/sin | solution.py:42
  67.4 9.6 %all-reduce.5 = (f32[8]{0:T(128)S(1)}, f32[7,7]{1,0:T(8,128)S(1)}, f32[8]{0:T(128)S(1)}) all-reduce(f32[8]{0:T(128)S(1)} %fusion.49, f32[7,7]{1,0:T(8,128)S(1)} %fusion.35, f32[8]{0:T(128)S(1)} %fusion.46), channel_id=1, replica_groups=mesh['col_0'=4,'col_1'=4,'col_2'=2,'grp'=4] {'col_0'}, use_global_device_ids=true, to_apply=%region_4.5 | all-reduce | flops 65 | bytes 520 | tf_op jit(solution)/shard_map/psum | solution.py:20
  77.0 9.9 %all-reduce.3 = (f32[8]{0:T(128)S(1)}, f32[7,7]{1,0:T(8,128)S(1)}, f32[8]{0:T(128)S(1)}) all-reduce(f32[8]{0:T(128)S(1)} %get-tuple-element.32, f32[7,7]{1,0:T(8,128)S(1)} %get-tuple-element.33, f32[8]{0:T(128)S(1)} %get-tuple-element.34), channel_id=1, replica_groups=mesh['col_0'=4,'col_1'=4,'col_2'=2,'grp'=4] {'col_1'}, use_global_device_ids=true, to_apply=%region_5.6 | all-reduce | flops 65 | bytes 520 | tf_op jit(solution)/shard_map/psum | solution.py:20
  86.9 6.9 %all-reduce.7 = (f32[8]{0:T(128)S(1)}, f32[7,7]{1,0:T(8,128)S(1)}, f32[8]{0:T(128)S(1)}) all-reduce(f32[8]{0:T(128)S(1)} %get-tuple-element.24, f32[7,7]{1,0:T(8,128)S(1)} %get-tuple-element.25, f32[8]{0:T(128)S(1)} %get-tuple-element.26), channel_id=1, replica_groups=mesh['col_0'=4,'col_1'=4,'col_2'=2,'grp'=4] {'col_2'}, use_global_device_ids=true, to_apply=%region_6.7 | all-reduce | flops 65 | bytes 520 | tf_op jit(solution)/shard_map/psum | solution.py:20
  93.7 18.5 %all-reduce.1 = (f32[8]{0:T(128)S(1)}, f32[7,7]{1,0:T(8,128)S(1)}, f32[8]{0:T(128)S(1)}) all-reduce(f32[8]{0:T(128)S(1)} %get-tuple-element.40, f32[7,7]{1,0:T(8,128)S(1)} %get-tuple-element.41, f32[8]{0:T(128)S(1)} %get-tuple-element.42), channel_id=1, replica_groups=mesh['col_0'=4,'col_1'=4,'col_2'=2,'grp'=4] {'grp'}, use_global_device_ids=true, to_apply=%region_7.8 | all-reduce | flops 65 | bytes 520 | tf_op jit(solution)/shard_map/psum | solution.py:20
  115.7 7.6 %multiply_reduce_fusion.3 = (f32[2,256,768]{2,1,0:T(8,128)S(1)}, f32[2,256,768]{2,1,0:T(8,128)S(1)}) fusion(bf16[1,2,256,768]{3,2,1,0:T(8,128)(2,1)} %get-tuple-element.56, f32[8]{0:T(128)S(1)} %convolution_bitcast_fusion.2, bf16[7,2,256,768]{3,2,1,0:T(8,128)(2,1)} %param.15, bf16[1,2,256,768]{3,2,1,0:T(8,128)(2,1)} %bitcast.126, ...), kind=kLoop, calls=%fused_computation.3 | loop fusion | flops 24379392 | bytes 15728672 | tf_op jit(solution)/shard_map/reduce_sum | solution.py:80
  123.4 2.6 fusion.32
  126.3 7.7 %fusion.22 = f32[1536,512]{1,0:T(8,128)S(1)} fusion(f32[512,768]{1,0:T(8,128)S(1)} %bitcast.122, f32[768,768]{1,0:T(8,128)S(1)} %copy-done.7, f32[768,768]{1,0:T(8,128)S(1)} %copy-done.9), kind=kOutput, calls=%fused_computation.35 | convolution fusion | flops 7250116608 | bytes 9437184 | tf_op jit(solution)/shard_map/dot_general | solution.py:48
  134.4 2.4 copy.30
  136.8 6.6 %all-to-all-start = ((f32[2,768,256]{2,0,1:T(2,128)}), f32[2,768,256]{2,0,1:T(2,128)}, u32[]{:S(2)}, u32[]{:S(2)}) async-start(f32[2,768,256]{2,0,1:T(2,128)} %copy.30), calls=%async_computation | async-start | bytes 3145728 | tf_op jit(solution)/shard_map/all_to_all | solution.py:141
  143.4 4.1 %multiply_convert_fusion.1 = (bf16[2,256,768]{2,1,0:T(8,128)(2,1)}, bf16[2,256,768]{2,1,0:T(8,128)(2,1)}, bf16[2,256,768]{2,1,0:T(8,128)(2,1)}) fusion(f32[256,768]{1,0:T(8,128)S(1)} %copy-done.12, f32[2,256,768]{2,1,0:T(8,128)} %get-tuple-element.43, f32[2,256,768]{2,1,0:T(8,128)} %copy-done.5), kind=kLoop, calls=%fused_computation.56 | loop fusion | flops 2359296 | bytes 6291456 | tf_op jit(solution)/shard_map/convert_element_type | solution.py:76
  147.5 2.6 concatenate.77
  150.1 2.6 reshape.207
  152.7 6.2 %fusion.19 = bf16[7,2,256,768]{3,2,1,0:T(8,128)(2,1)} fusion(bf16[7,2,256,768]{3,2,1,0:T(8,128)(2,1)} %param.16, bf16[1,2,256,768]{3,2,1,0:T(8,128)(2,1)} %bitcast.127), kind=kLoop, calls=%fused_computation.30 | loop fusion | flops 2752512 | bytes 11796480 | tf_op jit(solution)/shard_map/concatenate | solution.py:120
  160.1 3.5 %fusion.20 = bf16[7,2,256,768]{3,2,1,0:T(8,128)(2,1)} fusion(bf16[7,2,256,768]{3,2,1,0:T(8,128)(2,1)S(1)} %bitcast.124, bf16[1,2,256,768]{3,2,1,0:T(8,128)(2,1)S(1)} %copy-done.20), kind=kLoop, calls=%fused_computation.31 | loop fusion | flops 2752512 | bytes 11796480 | tf_op jit(solution)/shard_map/concatenate | solution.py:119
  163.6 1.4 reshape.209
  165.1 2.8 %pad_maximum_fusion.2 = bf16[7,2,256,768]{3,2,1,0:T(8,128)(2,1)S(1)} fusion(bf16[1,2,256,768]{3,2,1,0:T(8,128)(2,1)S(1)} %bitcast.128, bf16[7,2,256,768]{3,2,1,0:T(8,128)(2,1)} %copy-done), kind=kLoop, calls=%fused_computation.32 | loop fusion | flops 2752512 | bytes 11796480 | tf_op jit(solution)/shard_map/concatenate | solution.py:124
  167.9 5.8 %copy.43 = bf16[1,7,512,768]{3,1,2,0:T(8,128)(2,1)} copy(bf16[1,7,512,768]{3,2,1,0:T(8,128)(2,1)S(1)} %bitcast.125) | data formatting | bytes 11010048
  174.0 5.8 %copy.42 = bf16[1,7,512,768]{3,1,2,0:T(8,128)(2,1)S(1)} copy(bf16[1,7,512,768]{3,2,1,0:T(8,128)(2,1)} %bitcast.121) | data formatting | bytes 11010048
  179.8 4.5 %fusion.40 = f32[8]{0:T(128)S(1)} fusion(bf16[393216,1]{0,1:T(2,128)(2,1)S(1)} %copy-done.37, bf16[1,393216]{1,0:T(2,128)(2,1)S(1)} %copy-done.35, bf16[7,393216]{1,0:T(8,128)(2,1)S(1)} %bitcast.133), kind=kOutput, calls=%fused_computation.70 | convolution fusion | flops 18874368 | bytes 7077920 | tf_op jit(solution)/shard_map/dot_general | solution.py:67
  184.4 4.8 %fusion.43 = f32[8]{0:T(128)S(1)} fusion(bf16[393216,1]{0,1:T(2,128)(2,1)S(1)} %copy-done.34, bf16[1,393216]{1,0:T(2,128)(2,1)S(1)} %concatenate.71, bf16[7,393216]{1,0:T(8,128)(2,1)S(1)} %bitcast.134), kind=kOutput, calls=%fused_computation.71 | convolution fusion | flops 18874368 | bytes 7077920 | tf_op jit(solution)/shard_map/dot_general | solution.py:67
  189.2 9.4 %all-reduce.4 = (f32[8]{0:T(128)S(1)}, f32[8]{0:T(128)S(1)}, f32[]{:T(128)}, f32[]{:T(128)}, f32[]{:T(128)}) all-reduce(f32[8]{0:T(128)S(1)} %fusion.43, f32[8]{0:T(128)S(1)} %fusion.40, f32[]{:T(128)} %get-tuple-element.6, f32[]{:T(128)} %get-tuple-element.57, ...), channel_id=1, replica_groups=mesh['col_0'=4,'col_1'=4,'col_2'=2,'grp'=4] {'col_0'}, use_global_device_ids=true, to_apply=%region_16.19 | all-reduce | flops 19 | bytes 152 | tf_op jit(solution)/shard_map/psum | solution.py:20
  198.6 9.2 %all-reduce.2 = (f32[8]{0:T(128)S(1)}, f32[8]{0:T(128)S(1)}, f32[]{:T(128)}, f32[]{:T(128)}, f32[]{:T(128)}) all-reduce(f32[8]{0:T(128)S(1)} %get-tuple-element.27, f32[8]{0:T(128)S(1)} %get-tuple-element.28, f32[]{:T(128)} %get-tuple-element.29, ...), channel_id=1, replica_groups=mesh['col_0'=4,'col_1'=4,'col_2'=2,'grp'=4] {'col_1'}, use_global_device_ids=true, to_apply=%region_17.20 | all-reduce | flops 19 | bytes 152 | tf_op jit(solution)/shard_map/psum | solution.py:20
  207.8 7.2 %all-reduce.6 = (f32[8]{0:T(128)S(1)}, f32[8]{0:T(128)S(1)}, f32[]{:T(128)}, f32[]{:T(128)}, f32[]{:T(128)}) all-reduce(f32[8]{0:T(128)S(1)} %get-tuple-element.19, f32[8]{0:T(128)S(1)} %get-tuple-element.20, f32[]{:T(128)} %get-tuple-element.21, ...), channel_id=1, replica_groups=mesh['col_0'=4,'col_1'=4,'col_2'=2,'grp'=4] {'col_2'}, use_global_device_ids=true, to_apply=%region_18.21 | all-reduce | flops 19 | bytes 152 | tf_op jit(solution)/shard_map/psum | solution.py:20
  215.0 6.8 %all-reduce = (f32[8]{0:T(128)S(1)}, f32[8]{0:T(128)S(1)}, f32[]{:T(128)}, f32[]{:T(128)}, f32[]{:T(128)}) all-reduce(f32[8]{0:T(128)S(1)} %get-tuple-element.35, f32[8]{0:T(128)S(1)} %get-tuple-element.36, f32[]{:T(128)} %get-tuple-element.37, ...), channel_id=1, replica_groups=mesh['col_0'=4,'col_1'=4,'col_2'=2,'grp'=4] {'grp'}, use_global_device_ids=true, to_apply=%region_19.22 | all-reduce | flops 19 | bytes 152 | tf_op jit(solution)/shard_map/psum | solution.py:20
  225.2 6.7 %multiply_reduce_fusion.1 = (f32[2,256,768]{2,1,0:T(8,128)S(1)}, f32[2,256,768]{2,1,0:T(8,128)S(1)}) fusion(bf16[1,2,256,768]{3,2,1,0:T(8,128)(2,1)S(1)} %copy-done.30, bf16[7,2,256,768]{3,2,1,0:T(8,128)(2,1)} %fusion.20, f32[8]{0:T(128)S(1)} %convolution_bitcast_fusion, bf16[1,2,256,768]{3,2,1,0:T(8,128)(2,1)S(1)} %bitcast.129, ...), kind=kLoop, calls=%fused_computation.1 | loop fusion | flops 24379392 | bytes 15728672 | tf_op jit(solution)/shard_map/reduce_sum | solution.py:80
  232.5 1.6 copy-done.8
  234.9 7.7 %fusion.21 = f32[1536,512]{1,0:T(8,128)S(1)} fusion(f32[512,768]{1,0:T(8,128)S(1)} %bitcast.130, f32[768,768]{1,0:T(8,128)S(1)} %copy-done.8, f32[768,768]{1,0:T(8,128)S(1)} %copy-done.10), kind=kOutput, calls=%fused_computation.34 | convolution fusion | flops 7250116608 | bytes 9437184 | tf_op jit(solution)/shard_map/dot_general | solution.py:48
  243.0 2.4 copy.37
  245.3 5.8 %all-to-all-start.1 = ((f32[2,768,256]{2,0,1:T(2,128)}), f32[2,768,256]{2,0,1:T(2,128)S(1)}, u32[]{:S(2)}, u32[]{:S(2)}) async-start(f32[2,768,256]{2,0,1:T(2,128)} %copy.37), calls=%async_computation.1 | async-start | bytes 3145728 | tf_op jit(solution)/shard_map/all_to_all | solution.py:141
  254.4 2.3 copy.31
  256.7 1.4 stack.39
  258.1 15.8 %all-to-all-done.1 = f32[2,768,256]{2,0,1:T(2,128)S(1)} async-done(((f32[2,768,256]{2,0,1:T(2,128)}), f32[2,768,256]{2,0,1:T(2,128)S(1)}, u32[]{:S(2)}, u32[]{:S(2)}) %all-to-all-start.1) | async-done | bytes 1572896 | tf_op jit(solution)/shard_map/all_to_all | solution.py:141
  274.9 1.4 stack.43
  276.7 3.3 %pad_maximum_fusion.3 = f32[2,2,24,8192]{3,2,1,0:T(8,128)} fusion(f32[1,2,24,8192]{3,2,1,0:T(8,128)} %stack.43, f32[1,2,24,8192]{3,2,1,0:T(8,128)S(1)} %copy-done.29), kind=kLoop, calls=%fused_computation.37 | loop fusion | flops 786432 | bytes 6291456 | tf_op jit(solution)/shard_map/stack | solution.py:145
  (132 shorter events, 14.8 us)
Async XLA Ops:
  0.6 3.4 %copy-start.1 = (f32[2,256,768]{2,1,0:T(8,128)S(1)}, f32[2,256,768]{2,1,0:T(8,128)}, u32[]{:S(2)}) copy-start(f32[2,256,768]{2,1,0:T(8,128)} %param.11) | copy-start | bytes 4718596
  4.0 3.1 %copy-start.11 = (f32[256,768]{1,0:T(8,128)}, f32[256,768]{1,0:T(8,128)S(1)}, u32[]{:S(2)}) copy-start(f32[256,768]{1,0:T(8,128)S(1)} %get-tuple-element.59) | copy-start | bytes 2359300
  4.0 4.2 %copy-start.13 = (f32[2,256,768]{2,1,0:T(8,128)S(1)}, f32[2,256,768]{2,1,0:T(8,128)}, u32[]{:S(2)}) copy-start(f32[2,256,768]{2,1,0:T(8,128)} %param.13) | copy-start | bytes 4718596
  4.0 4.2 %copy-start.18 = (f32[256,768]{1,0:T(8,128)S(1)}, f32[256,768]{1,0:T(8,128)}, u32[]{:S(2)}) copy-start(f32[256,768]{1,0:T(8,128)} %param.14) | copy-start | bytes 2359300
  4.0 4.2 %copy-start.33 = (f32[2,256,768]{2,1,0:T(8,128)S(1)}, f32[2,256,768]{2,1,0:T(8,128)}, u32[]{:S(2)}) copy-start(f32[2,256,768]{2,1,0:T(8,128)} %param.12) | copy-start | bytes 4718596
  7.1 1.1 copy-start.5
  10.2 2.8 %copy-start.16 = (bf16[2,256,768]{2,1,0:T(8,128)(2,1)}, bf16[2,256,768]{2,1,0:T(8,128)(2,1)S(1)}, u32[]{:S(2)}) copy-start(bf16[2,256,768]{2,1,0:T(8,128)(2,1)S(1)} %get-tuple-element.49) | copy-start | bytes 2359300
  10.2 2.8 %copy-start.39 = (s32[256]{0:T(256)S(1)}, s32[256]{0:T(256)}, u32[]{:S(2)}) copy-start(s32[256]{0:T(256)} %param.17) | copy-start | bytes 3076
  14.1 6.8 %slice-start = ((s8[5505024]{0:T(1024)(128)(4,1)}), s8[1310720]{0:T(1024)(128)(4,1)S(1)}, s32[]{:S(2)}) async-start(s8[5505024]{0:T(1024)(128)(4,1)} %bitcast.117), calls=%async_computation.2 | async-start | bytes 2621440
  16.8 4.2 %slice-start.1 = ((s8[5505024]{0:T(1024)(128)(4,1)}), s8[4194304]{0:T(1024)(128)(4,1)S(1)}, s32[]{:S(2)}) async-start(s8[5505024]{0:T(1024)(128)(4,1)} %bitcast.117), calls=%async_computation.3 | async-start | bytes 8388608
  21.0 15.1 %copy-start = (bf16[7,2,256,768]{3,2,1,0:T(8,128)(2,1)}, bf16[7,2,256,768]{3,2,1,0:T(8,128)(2,1)S(1)}, u32[]{:S(2)}) copy-start(bf16[7,2,256,768]{3,2,1,0:T(8,128)(2,1)S(1)} %multiply_convert_fusion) | copy-start | bytes 16515076
  36.1 5.9 %copy-start.31 = (bf16[2,256,768]{2,1,0:T(8,128)(2,1)S(1)}, bf16[2,256,768]{2,1,0:T(8,128)(2,1)}, u32[]{:S(2)}) copy-start(bf16[2,256,768]{2,1,0:T(8,128)(2,1)} %get-tuple-element.47) | copy-start | bytes 2359300
  43.4 8.8 %copy-start.27 = (bf16[1,7,512,768]{3,1,2,0:T(8,128)(2,1)S(1)}, bf16[1,7,512,768]{3,1,2,0:T(8,128)(2,1)}, u32[]{:S(2)}) copy-start(bf16[1,7,512,768]{3,1,2,0:T(8,128)(2,1)} %copy.41) | copy-start | bytes 16515076
  43.4 8.8 %copy-start.36 = (bf16[1,393216]{1,0:T(2,128)(2,1)S(1)}, bf16[1,393216]{1,0:T(2,128)(2,1)}, u32[]{:S(2)}) copy-start(bf16[1,393216]{1,0:T(2,128)(2,1)} %concatenate.66) | copy-start | bytes 2359300
  43.4 8.8 %copy-start.38 = (bf16[393216,1]{0,1:T(2,128)(2,1)S(1)}, bf16[393216,1]{0,1:T(2,128)(2,1)}, u32[]{:S(2)}) copy-start(bf16[393216,1]{0,1:T(2,128)(2,1)} %reshape.201) | copy-start | bytes 2359300
  115.7 7.7 %copy-start.6 = (f32[2,256,768]{2,1,0:T(8,128)S(1)}, f32[2,256,768]{2,1,0:T(8,128)}, u32[]{:S(2)}) copy-start(f32[2,256,768]{2,1,0:T(8,128)} %copy-done.5) | copy-start | bytes 4718596
  115.7 7.7 %copy-start.12 = (f32[256,768]{1,0:T(8,128)S(1)}, f32[256,768]{1,0:T(8,128)}, u32[]{:S(2)}) copy-start(f32[256,768]{1,0:T(8,128)} %copy-done.11) | copy-start | bytes 2359300
  115.7 7.7 %copy-start.14 = (f32[2,256,768]{2,1,0:T(8,128)S(1)}, f32[2,256,768]{2,1,0:T(8,128)}, u32[]{:S(2)}) copy-start(f32[2,256,768]{2,1,0:T(8,128)} %param.13) | copy-start | bytes 4718596
  115.7 7.7 %copy-start.19 = (f32[256,768]{1,0:T(8,128)S(1)}, f32[256,768]{1,0:T(8,128)}, u32[]{:S(2)}) copy-start(f32[256,768]{1,0:T(8,128)} %param.14) | copy-start | bytes 2359300
  115.7 7.7 %copy-start.21 = (f32[256,768]{1,0:T(8,128)S(1)}, f32[256,768]{1,0:T(8,128)}, u32[]{:S(2)}) copy-start(f32[256,768]{1,0:T(8,128)} %get-tuple-element.58) | copy-start | bytes 2359300
  115.7 7.7 %copy-start.23 = (f32[256,768]{1,0:T(8,128)S(1)}, f32[256,768]{1,0:T(8,128)}, u32[]{:S(2)}) copy-start(f32[256,768]{1,0:T(8,128)} %fusion.53) | copy-start | bytes 2359300
  123.4 2.6 copy-start.7
  123.4 2.9 %copy-start.9 = (f32[768,768]{1,0:T(8,128)S(1)}, f32[768,768]{1,0:T(8,128)}, u32[]{:S(2)}) copy-start(f32[768,768]{1,0:T(8,128)} %get-tuple-element.61) | copy-start | bytes 7077892
  126.0 8.1 %copy-start.2 = (f32[2,256,768]{2,1,0:T(8,128)}, f32[2,256,768]{2,1,0:T(8,128)S(1)}, u32[]{:S(2)}) copy-start(f32[2,256,768]{2,1,0:T(8,128)S(1)} %get-tuple-element.44) | copy-start | bytes 4718596
  136.8 108.6 %all-to-all-start = ((f32[2,768,256]{2,0,1:T(2,128)}), f32[2,768,256]{2,0,1:T(2,128)}, u32[]{:S(2)}, u32[]{:S(2)}) async-start(f32[2,768,256]{2,0,1:T(2,128)} %copy.30), calls=%async_computation | async-start | bytes 3145728 | tf_op jit(solution)/shard_map/all_to_all | solution.py:141
  150.1 10.1 %slice-start.2 = ((s8[5505024]{0:T(1024)(128)(4,1)}), s8[1310720]{0:T(1024)(128)(4,1)S(1)}, s32[]{:S(2)}) async-start(s8[5505024]{0:T(1024)(128)(4,1)} %bitcast.123), calls=%async_computation.4 | async-start | bytes 2621440
  152.7 6.3 %copy-start.3 = (f32[2,256,768]{2,1,0:T(8,128)S(1)}, f32[2,256,768]{2,1,0:T(8,128)}, u32[]{:S(2)}) copy-start(f32[2,256,768]{2,1,0:T(8,128)} %copy-done.2) | copy-start | bytes 4718596
  152.7 7.4 %slice-start.3 = ((s8[5505024]{0:T(1024)(128)(4,1)}), s8[4194304]{0:T(1024)(128)(4,1)S(1)}, s32[]{:S(2)}) async-start(s8[5505024]{0:T(1024)(128)(4,1)} %bitcast.123), calls=%async_computation.5 | async-start | bytes 8388608
  158.9 1.2 copy-start.20
  160.1 3.5 %copy-start.32 = (bf16[2,256,768]{2,1,0:T(8,128)(2,1)S(1)}, bf16[2,256,768]{2,1,0:T(8,128)(2,1)}, u32[]{:S(2)}) copy-start(bf16[2,256,768]{2,1,0:T(8,128)(2,1)} %get-tuple-element.55) | copy-start | bytes 2359300
  163.6 1.4 copy-start.17
  167.9 5.8 %copy-start.25 = (bf16[2,256,768]{2,1,0:T(8,128)(2,1)S(1)}, bf16[2,256,768]{2,1,0:T(8,128)(2,1)}, u32[]{:S(2)}) copy-start(bf16[2,256,768]{2,1,0:T(8,128)(2,1)} %get-tuple-element.46) | copy-start | bytes 2359300
  173.9 5.9 %copy-start.28 = (bf16[1,7,512,768]{3,1,2,0:T(8,128)(2,1)S(1)}, bf16[1,7,512,768]{3,1,2,0:T(8,128)(2,1)}, u32[]{:S(2)}) copy-start(bf16[1,7,512,768]{3,1,2,0:T(8,128)(2,1)} %copy.43) | copy-start | bytes 16515076
  173.9 5.9 %copy-start.35 = (bf16[1,393216]{1,0:T(2,128)(2,1)S(1)}, bf16[1,393216]{1,0:T(2,128)(2,1)}, u32[]{:S(2)}) copy-start(bf16[1,393216]{1,0:T(2,128)(2,1)} %concatenate.77) | copy-start | bytes 2359300
  173.9 5.9 %copy-start.37 = (bf16[393216,1]{0,1:T(2,128)(2,1)S(1)}, bf16[393216,1]{0,1:T(2,128)(2,1)}, u32[]{:S(2)}) copy-start(bf16[393216,1]{0,1:T(2,128)(2,1)} %reshape.209) | copy-start | bytes 2359300
  179.8 4.6 %copy-start.34 = (bf16[393216,1]{0,1:T(2,128)(2,1)S(1)}, bf16[393216,1]{0,1:T(2,128)(2,1)}, u32[]{:S(2)}) copy-start(bf16[393216,1]{0,1:T(2,128)(2,1)} %reshape.207) | copy-start | bytes 2359300
  184.4 40.8 %copy-start.30 = (bf16[1,2,256,768]{3,2,1,0:T(8,128)(2,1)S(1)}, bf16[1,2,256,768]{3,2,1,0:T(8,128)(2,1)}, u32[]{:S(2)}) copy-start(bf16[1,2,256,768]{3,2,1,0:T(8,128)(2,1)} %fusion.55) | copy-start | bytes 2359300
  225.2 6.8 %copy-start.4 = (f32[2,256,768]{2,1,0:T(8,128)S(1)}, f32[2,256,768]{2,1,0:T(8,128)}, u32[]{:S(2)}) copy-start(f32[2,256,768]{2,1,0:T(8,128)} %copy-done.2) | copy-start | bytes 4718596
  225.2 6.8 %copy-start.15 = (f32[2,256,768]{2,1,0:T(8,128)S(1)}, f32[2,256,768]{2,1,0:T(8,128)}, u32[]{:S(2)}) copy-start(f32[2,256,768]{2,1,0:T(8,128)} %get-tuple-element.43) | copy-start | bytes 4718596
  225.2 6.8 %copy-start.22 = (f32[256,768]{1,0:T(8,128)S(1)}, f32[256,768]{1,0:T(8,128)}, u32[]{:S(2)}) copy-start(f32[256,768]{1,0:T(8,128)} %get-tuple-element.58) | copy-start | bytes 2359300
  225.2 6.8 %copy-start.24 = (f32[256,768]{1,0:T(8,128)S(1)}, f32[256,768]{1,0:T(8,128)}, u32[]{:S(2)}) copy-start(f32[256,768]{1,0:T(8,128)} %fusion.53) | copy-start | bytes 2359300
  232.0 2.1 copy-start.8
  232.0 2.9 %copy-start.10 = (f32[768,768]{1,0:T(8,128)S(1)}, f32[768,768]{1,0:T(8,128)}, u32[]{:S(2)}) copy-start(f32[768,768]{1,0:T(8,128)} %get-tuple-element.61) | copy-start | bytes 7077892
  232.5 10.1 %copy-start.26 = (f32[2,256,768]{2,1,0:T(8,128)}, f32[2,256,768]{2,1,0:T(8,128)S(1)}, u32[]{:S(2)}) copy-start(f32[2,256,768]{2,1,0:T(8,128)S(1)} %add_multiply_fusion) | copy-start | bytes 4718596
  245.3 28.6 %all-to-all-start.1 = ((f32[2,768,256]{2,0,1:T(2,128)}), f32[2,768,256]{2,0,1:T(2,128)S(1)}, u32[]{:S(2)}, u32[]{:S(2)}) async-start(f32[2,768,256]{2,0,1:T(2,128)} %copy.37), calls=%async_computation.1 | async-start | bytes 3145728 | tf_op jit(solution)/shard_map/all_to_all | solution.py:141
  274.9 1.8 copy-start.29
where the time goes:
time: 285 us; the launch traced here: 280 us
  blocking collectives  77.4 us (27%)
  other arithmetic  68.6 us (24%)
  local copies, waits for them, and re-layouts  53 us (19%)
  matrix products  48 us (17%)
  waiting for transfers between devices  15.8 us (6%)
  starting transfers between devices  12.5 us (4%)
  between operations  4.82 us (2%)
    psum x8, blocking collectives, by_axis(): array = lax.psum(array, axis)  77.4 us
    dot_general x5, matrix products, inner_rows(): lax.dot_general(flatten_rows(first_stack), flatten_rows(second_stack), ((...  32.1 us
    unnamed x92, local copies, waits for them, and re-layouts  27.7 us
    all_to_all x2, waiting for transfers between devices, body(): lax.all_to_all(slabs, COL, split_axis=1, concat_axis=2, tiled=True)  15.8 us
    dot_general x2, matrix products, to_planes(): lax.dot_general(dft_table, stacked_rows, (((1,), (1,)), ((), ())), precis...  15.4 us
    reduce_sum x2, other arithmetic, combine_history(): jnp.sum(coefficients[:, None, None, None] * stack.astype(jnp.float32), ax...  14.3 us
    all_to_all x2, starting transfers between devices, body(): lax.all_to_all(slabs, COL, split_axis=1, concat_axis=2, tiled=True)  12.5 us
    sin x1, other arithmetic, plane_table(): return jnp.concatenate([jnp.cos(angle), jnp.sin(angle)], axis=0) * spread  10.6 us
  transfers between devices with their start and end apart: 2, of which 1 were waited for; matrix products, arithmetic and copies ran while one was open for 25% of the time, Pallas kernels for 0%

commit v1 on v0

v1 whole, which is shorter than its diff:
```python
import functools
import math

import jax
import jax.numpy as jnp
import numpy as np
from jax import lax
from jax.experimental import pallas as pl
from jax.experimental.pallas import tpu as pltpu
from jax.sharding import PartitionSpec as P

HIST = 8
ITERS = 2
MIXING = 0.7
NZ = 768
COLS = 256
N_COL = 32
N_GRP = 4
ZB = NZ // N_COL
HALF = COLS // 2
CUT2 = (NZ // 2 - 1) ** 2
CH = 32
N_CH = COLS // CH
SUB = 16
PEAK = 255.0 / 128.0
SCALE = 1.0 / (math.sqrt(NZ) * PEAK)
MESH = pl.DeviceIdType.MESH
F32 = jnp.float32
BF16 = jnp.bfloat16


def plane_table():
    k = np.arange(NZ)
    angle = (k[:, None] * k[None, :] % NZ) * (2.0 * math.pi / NZ)
    both = np.concatenate([np.cos(angle), np.sin(angle)], axis=1) * PEAK
    return jnp.asarray(both.astype(np.float32)).astype(BF16)


def nt_dot(left, right, precision=None):
    return lax.dot_general(
        left, right, (((1,), (1,)), ((), ())), precision=precision, preferred_element_type=F32
    )


def kernel(
    dn_h, db_h, src_h, resp_h, hd_h, hr_h, cs_s, scr_s, tab_h,
    slab_o, mix_o, norm_o,
    dn, db, src, resp, hd, hr, tab, d1, met, pre, w, w2, acc, acc2, sq, fold, amat, cvec,
    rmat, prod, pay, got,
    load_sem, late_sem, tab_sem, own_sem, send_sem, recv_sem, rsend_sem, rrecv_sem,
):
    col, grp = lax.axis_index("col"), lax.axis_index("grp")
    me = col * N_GRP + grp
    y0, z0, c0 = col // 8, (col // 2) % 4, col % 2

    def early(ch):
        rows = pl.ds(pl.multiple_of(ch * CH, CH), CH)
        return [
            pltpu.make_async_copy(dn_h.at[:, rows], dn.at[:, rows], load_sem.at[ch]),
            pltpu.make_async_copy(db_h.at[:, rows], db.at[:, rows], load_sem.at[ch]),
            pltpu.make_async_copy(src_h.at[:, rows], src.at[:, rows], load_sem.at[ch]),
            pltpu.make_async_copy(resp_h.at[rows], resp.at[rows], load_sem.at[ch]),
            pltpu.make_async_copy(hr_h.at[:, :, rows], hr.at[0:7, :, rows], load_sem.at[ch]),
        ]

    for ch in range(N_CH):
        for copy in early(ch):
            copy.start()
    late = pltpu.make_async_copy(hd_h, hd.at[0:7], late_sem)
    late.start()
    table = pltpu.make_async_copy(tab_h, tab, tab_sem)
    table.start()

    barrier = pltpu.get_barrier_semaphore()

    def peer(s):
        y = (y0 + 2 + s // 32) % 4
        z = (z0 + 2 + (s // 8) % 4) % 4
        x = (grp + 2 + (s // 2) % 4) % 4
        c = (c0 + s) % 2
        return y * 8 + z * 2 + c, x

    def others(body):
        def step(s, carry):
            body(*peer(s + (s >= 84).astype(jnp.int32)))
            return carry

        lax.fori_loop(0, 127, step, 0)

    others(
        lambda a, g: pl.semaphore_signal(barrier, inc=1, device_id=(a, g), device_id_type=MESH)
    )

    screen = scr_s[0]
    lane = lax.broadcasted_iota(jnp.int32, (8, NZ), 1)
    signed = jnp.where(lane < NZ // 2, lane, lane - NZ)
    signed2 = signed * signed
    row128 = lax.broadcasted_iota(jnp.int32, (8, 128), 0)
    lane128 = lax.broadcasted_iota(jnp.int32, (8, 128), 1)
    sq[...] = jnp.zeros_like(sq)
    acc[...] = jnp.zeros_like(acc)
    w2[...] = jnp.zeros_like(w2)
    acc2[...] = jnp.zeros_like(acc2)

    def geometry(i, total):
        base = pl.multiple_of(i * 8, 8)
        column = jnp.zeros((8, 128), jnp.int32)
        for r in range(8):
            column = jnp.where(row128 == r, cs_s[base + r], column)
        squared = jnp.concatenate([column] * (NZ // 128), axis=1) + signed2
        shells = squared.astype(F32)
        ratio = (shells + screen) / shells
        metric = jnp.where(squared <= CUT2, ratio, 0.0)
        met[pl.ds(base, 8)] = metric
        pre[pl.ds(base, 8)] = MIXING * shells / (shells + screen)
        return total + metric

    weight_rows = lax.fori_loop(0, COLS // 8, geometry, jnp.zeros((8, NZ), F32))

    def first(ch, carry):
        for copy in early(ch):
            copy.wait()
        for u in range(CH // SUB):
            rows = pl.ds(pl.multiple_of(ch * CH + u * SUB, SUB), SUB)
            metric = met[rows]
            r = resp[rows]
            for p in range(2):
                s = src[p, rows]
                residual = s - r * dn[p, rows]
                earlier = s - r * db[p, rows]
                hd[7, p, rows] = (dn[p, rows] - db[p, rows]).astype(BF16)
                hr[7, p, rows] = (residual - earlier).astype(BF16)
                hr[8, p, rows] = residual.astype(BF16)
                sq[...] += metric * residual * residual
                for i in range(HIST):
                    value = hr[i, p, rows].astype(F32)
                    w[p, i * CH + u * SUB : i * CH + (u + 1) * SUB] = (metric * value).astype(BF16)
        rows = pl.ds(pl.multiple_of(ch * CH, CH), CH)
        total = acc[...]
        for p in range(2):
            total = total + nt_dot(hr[:, p, rows].reshape(9 * CH, NZ), w[p])
        acc[...] = total
        return carry

    lax.fori_loop(0, N_CH, first, 0)

    def fold3(rows):
        return rows[:, :256] + rows[:, 256:512] + rows[:, 512:]

    def group_sums(lanes):
        l = lax.broadcasted_iota(jnp.int32, (lanes, 128), 0)
        j = lax.broadcasted_iota(jnp.int32, (lanes, 128), 1)
        return jnp.where(l // CH == j, 1.0, 0.0).astype(F32)

    def diagonal(total):
        r = lax.broadcasted_iota(jnp.int32, total.shape, 0)
        l = lax.broadcasted_iota(jnp.int32, total.shape, 1)
        kept = jnp.where(r % CH == l % CH, total, 0.0)
        return jnp.sum(kept.reshape(total.shape[0] // CH, CH, total.shape[1]), axis=1)

    def pack(slot, groups):
        ones = group_sums(groups)
        both = lax.dot_general(
            fold[:, :groups], ones, (((1,), (0,)), ((), ())),
            precision=lax.Precision.HIGHEST, preferred_element_type=F32,
        )
        upper = pltpu.roll(both[:8], 0, 1, stride=8, stride_axis=0)
        lower = pltpu.roll(both[8:], 64, 1, stride=8, stride_axis=0)
        row = jnp.sum(upper + lower, axis=0, keepdims=True)
        pay[slot] = row
        got[slot, pl.ds(me, 1)] = row.reshape(1, 1, 128)

    def spread(slot):
        def go(a, g):
            pltpu.make_async_remote_copy(
                src_ref=pay.at[slot],
                dst_ref=got.at[slot, me],
                send_sem=rsend_sem.at[slot],
                recv_sem=rrecv_sem.at[slot],
                device_id=(a, g),
                device_id_type=MESH,
            ).start()

        others(go)

    def gathered(slot):
        whole = got.at[slot, 0:127]
        pltpu.make_async_copy(whole, whole, rsend_sem.at[slot]).wait()
        pltpu.make_async_copy(whole, whole, rrecv_sem.at[slot]).wait()
        return jnp.sum(got[slot].reshape(128, 128), axis=0, keepdims=True)

    def unpack(row):
        same = jnp.broadcast_to(row, (8, 128))
        out = same
        for i in range(1, 8):
            out = jnp.where(row128 == i, pltpu.roll(same, 128 - 8 * i, 1), out)
        return out

    def lanes_sum(row, start):
        lanes = lax.broadcasted_iota(jnp.int32, (1, 128), 1)
        kept = jnp.where((lanes >= start) & (lanes < start + 8), row, 0.0)
        return jnp.sum(kept, axis=1, keepdims=True)

    def flip(matrix):
        out = jnp.zeros((8, 128), F32)
        for j in range(8):
            row = jnp.broadcast_to(matrix[j : j + 1], (8, 128))
            column = jnp.sum(jnp.where(row128 == lane128, row, 0.0), axis=1, keepdims=True)
            out = jnp.where(lane128 == j, column, out)
        return out

    def solve(matrix, right):
        m = jnp.where(lane128 < 8, matrix, jnp.where(lane128 == 8, right, 0.0))
        for k in range(8):
            row = m[k : k + 1] / m[k : k + 1, k : k + 1]
            m = jnp.where(row128 == k, row, m - m[:, k : k + 1] * row)
        return jnp.broadcast_to(m[:, 8:9], (8, NZ))

    fold[...] = jnp.zeros_like(fold)
    fold[0:9] = diagonal(acc[...])
    fold[9:10] = fold3(jnp.sum(sq[...], axis=0, keepdims=True))
    fold[10:11] = fold3(jnp.sum(weight_rows, axis=0, keepdims=True))
    pl.semaphore_wait(barrier, 127)
    pack(0, 256)
    spread(0)
    late.wait()
    table.wait()
    row = gathered(0)
    margin = unpack(row)
    margin = 0.5 * (margin + flip(margin))
    amat[...] = jnp.where(lane128 < 8, margin, 0.0)
    lanes8 = jnp.broadcast_to(pltpu.roll(row, 64, 1), (8, 128))
    right = jnp.sum(jnp.where(row128 == lane128, lanes8, 0.0), axis=1, keepdims=True)
    weight_total = lanes_sum(row, 80)
    norm0 = jnp.sqrt(lanes_sum(row, 72) / weight_total)
    cvec[...] = solve(amat[...], right)

    def mix(t, h, old, new):
        def step(i, carry):
            local = pl.multiple_of(i * SUB, SUB)
            rows = pl.ds(pl.multiple_of(h * HALF + i * SUB, SUB), SUB)
            r = resp[rows]
            inside = met[rows] > 0.0
            precond = pre[rows]
            values = []
            for p in range(2):
                density = old[p, rows]
                rho = density
                res = src[p, rows] - r * density
                for j in range(HIST):
                    c = cvec[j : j + 1]
                    rho = rho - c * hd[t + j, p, rows].astype(F32)
                    res = res - c * hr[t + j, p, rows].astype(F32)
                mixed = jnp.where(inside, rho + precond * res, 0.0)
                new[p, rows] = mixed
                values.append(mixed * SCALE)
            re, im = values[0].astype(BF16), values[1].astype(BF16)
            rmat[pl.ds(local, SUB), :NZ] = re
            rmat[pl.ds(local, SUB), NZ:] = (-values[1]).astype(BF16)
            rmat[pl.ds(HALF + local, SUB), :NZ] = im
            rmat[pl.ds(HALF + local, SUB), NZ:] = re
            return carry

        lax.fori_loop(0, HALF // SUB, step, 0)
        planes = nt_dot(tab[...], rmat[...])
        prod[t, h, 0] = planes[:, :HALF]
        prod[t, h, 1] = planes[:, HALF:]

    def out_block(t, h):
        return slab_o.at[t, :, :, pl.ds(pl.multiple_of(col * COLS + h * HALF, HALF), HALF)]

    def block(t, h, a):
        return prod.at[t, h, :, pl.ds(pl.multiple_of(a * ZB, 8), ZB)]

    def send(t, h):
        def step(s, carry):
            pair = s // 2
            z = (z0 + pair) % 4
            y = (y0 + pair // 4 + pair) % 4
            a = y * 8 + z * 2 + (c0 + s) % 2
            pltpu.make_async_remote_copy(
                src_ref=block(t, h, a),
                dst_ref=out_block(t, h),
                send_sem=send_sem.at[t],
                recv_sem=recv_sem.at[t],
                device_id=(a, grp),
                device_id_type=MESH,
            ).start()
            return carry

        lax.fori_loop(1, N_COL, step, 0)
        pltpu.make_async_copy(block(t, h, col), out_block(t, h), own_sem).start()

    def finish(t):
        for h in range(2):
            pltpu.make_async_copy(block(t, h, col), out_block(t, h), own_sem).wait()
        rows = (N_COL - 1) * COLS
        whole = slab_o.at[t, :, :, 0:rows]
        pltpu.make_async_copy(whole, whole, send_sem.at[t]).wait()
        pltpu.make_async_copy(whole, whole, recv_sem.at[t]).wait()

    mix(0, 0, dn, d1)
    send(0, 0)
    mix(0, 1, dn, d1)

    sq[...] = jnp.zeros_like(sq)

    def second(ch, carry):
        for u in range(CH // SUB):
            rows = pl.ds(pl.multiple_of(ch * CH + u * SUB, SUB), SUB)
            metric = met[rows]
            r = resp[rows]
            for p in range(2):
                s = src[p, rows]
                residual = s - r * d1[p, rows]
                earlier = s - r * dn[p, rows]
                hd[8, p, rows] = (d1[p, rows] - dn[p, rows]).astype(BF16)
                newest = (residual - earlier).astype(BF16)
                hr[8, p, rows] = newest
                sq[...] += metric * residual * residual
                half = residual.astype(BF16).astype(F32)
                w2[p, u * SUB : (u + 1) * SUB] = (metric * newest.astype(F32)).astype(BF16)
                w2[p, CH + u * SUB : CH + (u + 1) * SUB] = (metric * half).astype(BF16)
        rows = pl.ds(pl.multiple_of(ch * CH, CH), CH)
        total = acc2[...]
        for p in range(2):
            total = total + nt_dot(hr[1:9, p, rows].reshape(8 * CH, NZ), w2[p])
        acc2[...] = total
        return carry

    lax.fori_loop(0, N_CH, second, 0)
    fold[...] = jnp.zeros_like(fold)
    fold[0:8, 0:128] = diagonal(acc2[...])
    squares = fold3(jnp.sum(sq[...], axis=0, keepdims=True))
    fold[8:9, 0:128] = squares[:, :128] + squares[:, 128:]
    pack(1, 128)
    spread(1)
    send(0, 1)
    row = gathered(1)
    table1 = unpack(row)
    newest = table1[:, 0:1]
    across = jnp.sum(jnp.where(row128 == lane128, newest, 0.0), axis=0, keepdims=True)
    shifted = pltpu.roll(pltpu.roll(amat[...], 7, 0), 127, 1)
    matrix = jnp.where(lane128 == 7, newest, jnp.where(row128 == 7, across, shifted))
    norm1 = jnp.sqrt(lanes_sum(row, 64) / weight_total)
    cvec[...] = solve(matrix, table1[:, 1:2])

    mix(1, 0, d1, mix_o)
    send(1, 0)
    mix(1, 1, d1, mix_o)
    send(1, 1)
    lanes = lax.broadcasted_iota(jnp.int32, (1, 128), 1)
    norm_o[...] = jnp.where(lanes == 0, norm0, jnp.where(lanes == 1, norm1, 0.0))
    finish(0)
    finish(1)


def deliver(slab_v, mix_v, norm_v, slab_o, mix_o, norm_o, sem):
    copies = (
        pltpu.make_async_copy(slab_v, slab_o, sem.at[0]),
        pltpu.make_async_copy(mix_v, mix_o, sem.at[1]),
    )
    for copy in copies:
        copy.start()
    lanes = lax.broadcasted_iota(jnp.int32, (1, 128), 1)
    for t in range(ITERS):
        norm_o[t] = jnp.sum(jnp.where(lanes == t, norm_v[...], 0.0))
    for copy in copies:
        copy.wait()


def body(dn, db, src, resp, hd, hr, shell, screening):
    any_spec = pl.BlockSpec(memory_space=pl.ANY)
    hbm = pl.BlockSpec(memory_space=pltpu.HBM)
    smem = pl.BlockSpec(memory_space=pltpu.SMEM)
    stack = (2, COLS, NZ)
    vmem = pl.BlockSpec(memory_space=pltpu.VMEM)
    slab_shape = (ITERS, 2, ZB, N_COL * COLS)
    parts = pl.pallas_call(
        kernel,
        out_shape=(pltpu.VMEM(slab_shape, F32), pltpu.VMEM(stack, F32), pltpu.VMEM((1, 128), F32)),
        in_specs=[hbm] * 6 + [smem, smem, hbm],
        out_specs=(vmem, vmem, vmem),
        scratch_shapes=[
            pltpu.VMEM(stack, F32),
            pltpu.VMEM(stack, F32),
            pltpu.VMEM(stack, F32),
            pltpu.VMEM((COLS, NZ), F32),
            pltpu.VMEM((9,) + stack, BF16),
            pltpu.VMEM((9,) + stack, BF16),
            pltpu.VMEM((NZ, 2 * NZ), BF16),
            pltpu.VMEM(stack, F32),
            pltpu.VMEM((COLS, NZ), F32),
            pltpu.VMEM((COLS, NZ), F32),
            pltpu.VMEM((2, HIST * CH, NZ), BF16),
            pltpu.VMEM((2, 128, NZ), BF16),
            pltpu.VMEM((9 * CH, HIST * CH), F32),
            pltpu.VMEM((8 * CH, 128), F32),
            pltpu.VMEM((SUB, NZ), F32),
            pltpu.VMEM((16, 256), F32),
            pltpu.VMEM((8, 128), F32),
            pltpu.VMEM((8, NZ), F32),
            pltpu.VMEM((COLS, 2 * NZ), BF16),
            pltpu.VMEM((ITERS, 2, 2, NZ, HALF), F32),
            pltpu.VMEM((2, 1, 128), F32),
            pltpu.VMEM((2, N_COL * N_GRP, 1, 128), F32),
            pltpu.SemaphoreType.DMA((N_CH,)),
            pltpu.SemaphoreType.DMA,
            pltpu.SemaphoreType.DMA,
            pltpu.SemaphoreType.DMA,
            pltpu.SemaphoreType.DMA((ITERS,)),
            pltpu.SemaphoreType.DMA((ITERS,)),
            pltpu.SemaphoreType.DMA((2,)),
            pltpu.SemaphoreType.DMA((2,)),
        ],
        compiler_params=pltpu.CompilerParams(
            collective_id=0, has_side_effects=True, vmem_limit_bytes=54 * 1024 * 1024
        ),
        name="mixing",
    )(dn, db, src, resp, hd, hr, shell, screening, plane_table())
    return pl.pallas_call(
        deliver,
        out_shape=(
            jax.ShapeDtypeStruct(slab_shape, F32),
            jax.ShapeDtypeStruct(stack, F32),
            jax.ShapeDtypeStruct((ITERS,), F32),
        ),
        in_specs=[vmem, vmem, vmem],
        out_specs=(any_spec, any_spec, smem),
        scratch_shapes=[pltpu.SemaphoreType.DMA((2,))],
        compiler_params=pltpu.CompilerParams(vmem_limit_bytes=16 * 1024 * 1024),
        name="deliver",
    )(*parts)


def solution(mesh):
    columns = ("col", "grp")
    return jax.shard_map(
        body,
        mesh=mesh,
        in_specs=(
            P(None, columns, None),
            P(None, columns, None),
            P(None, columns, None),
            P(columns, None),
            P(None, None, columns, None),
            P(None, None, columns, None),
            P(columns),
            P(),
        ),
        out_specs=(P(None, None, "col", "grp"), P(None, columns, None), P()),
        check_vma=False,
    )
```

time: 285 us -> 75.9 us (0.27); the launches traced: 280 us -> 75.8 us
  blocking collectives: 77.4 us -> 0 us
  Pallas kernels: 0 us -> 74.5 us
  other arithmetic: 68.6 us -> 0 us
  local copies, waits for them, and re-layouts: 53 us -> 0 us
  matrix products: 48 us -> 0 us
  waiting for transfers between devices: 15.8 us -> 0 us
  starting transfers between devices: 12.5 us -> 0 us
  between operations: 4.82 us -> 1.29 us
    psum x8 -> x0, blocking collectives: 77.4 us -> none  [by_axis(): array = lax.psum(array, axis)]
    pallas_call x0 -> x2, Pallas kernels: none -> 74.5 us  [the longest x1 71.8 us: body(): pl.pallas_call(kernel, out_shape=(pltpu.VMEM(slab_shape, F32), pltpu.VMEM...]
    dot_general x7 -> x0, matrix products: 47.5 us -> none  [the longest x5 32.1 us: inner_rows(): lax.dot_general(flatten_rows(first_stack), flatten_rows(second_stack), ((...]
    unnamed x92 -> x0, local copies, waits for them, and re-layouts: 27.7 us -> none
    reduce_sum x4 -> x0, other arithmetic: 19.5 us -> none  [the longest x2 14.3 us: combine_history(): jnp.sum(coefficients[:, None, None, None] * stack.astype(jnp.float32), ax...]
    all_to_all x2 -> x0, waiting for transfers between devices: 15.8 us -> none  [body(): lax.all_to_all(slabs, COL, split_axis=1, concat_axis=2, tiled=True)]
    another operation x8 -> x0, local copies, waits for them, and re-layouts: 14.5 us -> none
    convert_element_type x5 -> x0, other arithmetic: 14.3 us -> none  [the longest x3 10.2 us: apply_metric(): return (metric[None, None] * stack.astype(jnp.float32)).astype(jnp.bfloat16)]
  transfers between devices with their start and end apart: 2 -> 0, of which waited for: 1 -> 0; matrix products, arithmetic and copies ran while one was open for 25% -> 0% of each run, Pallas kernels for 0% -> 0%
where the time goes in v1:
time: 75.9 us; the launch traced here: 75.8 us
  Pallas kernels  74.5 us (98%)
  between operations  1.29 us (2%)
    pallas_call x1, Pallas kernels, body(): pl.pallas_call(kernel, out_shape=(pltpu.VMEM(slab_shape, F32), pltpu.VMEM...  71.8 us
    pallas_call x1, Pallas kernels, body(): pl.pallas_call(deliver, out_shape=(jax.ShapeDtypeStruct(slab_shape, F32),...  2.71 us

profile of v1, /device:TPU:1, one launch (start us, length us, event | category | flops | bytes accessed | tf_op | source)
XLA Modules:
  0.0 75.8 jit_solution(8984785494971413601)
XLA Ops:
  1.3 71.8 %mixing.1 = (f32[2,2,24,8192]{3,2,1,0:T(8,128)S(1)}, f32[2,256,768]{2,1,0:T(8,128)S(1)}, f32[1,128]{1,0:T(1,128)S(1)}) custom-call(f32[2,256,768]{2,1,0:T(8,128)} %dn_h.1, f32[2,256,768]{2,1,0:T(8,128)} %db_h.1, f32[2,256,768]{2,1,0:T(8,128)} %src_h.1, f32[256,768]{1,0:T(8,128)} %resp_h.1, bf16[7,2,256,768]{3,2,1,0:T(8,128)(2,1)} %hd_h.1, ...), custom_call_target="tpu_custom_call" | custom-call | tf_op jit(solution)/shard_map/mixing/pallas_call | solution.py:379
  73.1 2.7 %deliver.1 = (f32[2,2,24,8192]{3,2,1,0:T(8,128)}, f32[2,256,768]{2,1,0:T(8,128)}, f32[2]{0:T(128)}) custom-call(f32[2,2,24,8192]{3,2,1,0:T(8,128)S(1)} %get-tuple-element.6.slab_v, f32[2,256,768]{2,1,0:T(8,128)S(1)} %get-tuple-element.7.mix_v, f32[1,128]{1,0:T(1,128)S(1)} %get-tuple-element.8.norm_v), custom_call_target="tpu_custom_call" | custom-call | tf_op jit(solution)/shard_map/deliver/pallas_call | solution.py:421

commit v2 on v1

v2 whole, which is shorter than its diff:
```python
import functools
import math

import jax
import jax.numpy as jnp
import numpy as np
from jax import lax
from jax.experimental import pallas as pl
from jax.experimental.pallas import tpu as pltpu
from jax.sharding import PartitionSpec as P

HIST = 8
ITERS = 2
MIXING = 0.7
NZ = 768
COLS = 256
N_COL = 32
N_GRP = 4
ZB = NZ // N_COL
HALF = COLS // 2
CUT2 = (NZ // 2 - 1) ** 2
CH = 32
N_CH = COLS // CH
SUB = 16
PEAK = 255.0 / 128.0
SCALE = 1.0 / (math.sqrt(NZ) * PEAK)
MESH = pl.DeviceIdType.MESH
F32 = jnp.float32
BF16 = jnp.bfloat16


def plane_table():
    k = np.arange(NZ)
    angle = (k[:, None] * k[None, :] % NZ) * (2.0 * math.pi / NZ)
    both = np.concatenate([np.cos(angle), np.sin(angle)], axis=1) * PEAK
    return jnp.asarray(both.astype(np.float32)).astype(BF16)


def nt_dot(left, right, precision=None):
    return lax.dot_general(
        left, right, (((1,), (1,)), ((), ())), precision=precision, preferred_element_type=F32
    )


def kernel(
    dn_h, db_h, src_h, resp_h, hd_h, hr_h, cs_h, scr_h, tab_h,
    slab_o, mix_o, norm_o,
    cs_m, scr_m, dn, db, src, resp, hd, hr, hn, tab, d1, met, pre, base, step, w0, w1, x0, x1, w2, acc, sq, weights,
    fold, amat, cvec, rmat, prod, whole, pay, gota,
    small_sem, load_sem, late_sem, tab_sem, own_sem, send_sem, recv_sem, rsend_sem, rrecv_sem,
):
    col, grp = lax.axis_index("col"), lax.axis_index("grp")
    ys = [(col // 8 + d) % 4 * 8 for d in range(4)]
    zs = [(col // 2 + d) % 4 * 2 for d in range(4)]
    cs = [col % 2, (col + 1) % 2]
    place = {1: 0, 3: 1, 2: 2, 0: 3}
    near = [(1, 2), (3, 2), (1, 1), (3, 3), (1, 3), (3, 1), (1, 0), (3, 0)]
    far = [(2, 2), (0, 2), (2, 1), (2, 3), (2, 0), (0, 1), (0, 3), (0, 0)]
    last = [
        (2, 2), (2, 1), (2, 3), (1, 2), (3, 2), (2, 0), (0, 2), (1, 1),
        (3, 3), (1, 3), (3, 1), (0, 0), (1, 0), (3, 0), (0, 1), (0, 3),
    ]
    others_all = [
        (ys[dy] + zs[dz] + cs[dc], (grp + dx) % 4)
        for dy in (2, 1, 3, 0) for dz in (2, 1, 3, 0) for dx in (2, 1, 3, 0) for dc in (1, 0)
        if dx or dy or dz or dc
    ]
    def early(ch):
        rows = pl.ds(pl.multiple_of(ch * CH, CH), CH)
        return [
            pltpu.make_async_copy(dn_h.at[:, rows], dn.at[:, rows], load_sem.at[ch]),
            pltpu.make_async_copy(db_h.at[:, rows], db.at[:, rows], load_sem.at[ch]),
            pltpu.make_async_copy(src_h.at[:, rows], src.at[:, rows], load_sem.at[ch]),
            pltpu.make_async_copy(resp_h.at[rows], resp.at[rows], load_sem.at[ch]),
            pltpu.make_async_copy(hr_h.at[:, :, rows], hr.at[:, :, rows], load_sem.at[ch]),
        ]

    small = [
        pltpu.make_async_copy(cs_h, cs_m, small_sem.at[0]),
        pltpu.make_async_copy(scr_h, scr_m, small_sem.at[1]),
    ]
    for copy in small:
        copy.start()
    for ch in range(N_CH):
        for copy in early(ch):
            copy.start()
    late = pltpu.make_async_copy(hd_h, hd, late_sem)
    table = [
        pltpu.make_async_copy(
            tab_h.at[pl.ds(pl.multiple_of(ys[dy] * ZB, 8 * ZB), 8 * ZB)],
            tab.at[place[dy] * 8 * ZB : (place[dy] + 1) * 8 * ZB],
            tab_sem.at[dy],
        )
        for dy in range(4)
    ]

    barrier = pltpu.get_barrier_semaphore()
    for peer in others_all:
        pl.semaphore_signal(barrier, inc=1, device_id=peer, device_id_type=MESH)

    for copy in small:
        copy.wait()
    screen = scr_m[0]
    lane = lax.broadcasted_iota(jnp.int32, (8, NZ), 1)
    signed = jnp.where(lane < NZ // 2, lane, lane - NZ)
    signed2 = signed * signed
    row128 = lax.broadcasted_iota(jnp.int32, (8, 128), 0)
    lane128 = lax.broadcasted_iota(jnp.int32, (8, 128), 1)
    sq[...] = jnp.zeros_like(sq)
    acc[...] = jnp.zeros_like(acc)
    weights[...] = jnp.zeros_like(weights)

    def geometry(first_row):
        column = jnp.zeros((8, 128), jnp.int32)
        for r in range(8):
            column = jnp.where(row128 == r, cs_m[first_row + r], column)
        squared = jnp.concatenate([column] * (NZ // 128), axis=1) + signed2
        shells = squared.astype(F32)
        metric = jnp.where(squared <= CUT2, (shells + screen) / shells, 0.0)
        met[pl.ds(first_row, 8)] = metric
        pre[pl.ds(first_row, 8)] = MIXING * shells / (shells + screen)
        weights[...] += metric

    def weigh(ch, w, x):
        for copy in early(ch):
            copy.wait()
        for u in range(CH // 8):
            geometry(pl.multiple_of(ch * CH + u * 8, 8))
        for u in range(CH // SUB):
            rows = pl.ds(pl.multiple_of(ch * CH + u * SUB, SUB), SUB)
            here = slice(u * SUB, (u + 1) * SUB)
            metric = met[rows]
            r = resp[rows]
            for p in range(2):
                s = src[p, rows]
                residual = s - r * dn[p, rows]
                earlier = s - r * db[p, rows]
                newest = (residual - earlier).astype(BF16)
                hn[0, p, rows] = newest
                x[p, here] = newest
                x[p, CH + u * SUB : CH + (u + 1) * SUB] = residual.astype(BF16)
                sq[...] += metric * residual * residual
                for i in range(HIST):
                    value = (hr[i, p, rows] if i < HIST - 1 else newest).astype(F32)
                    w[p, i * CH + u * SUB : i * CH + (u + 1) * SUB] = (metric * value).astype(BF16)

    def multiply(ch, w, x):
        rows = pl.ds(pl.multiple_of(ch * CH, CH), CH)
        for p in range(2):
            pairs = [hr[:, p, rows].reshape(7 * CH, NZ), x[p]]
            acc[p] = acc[p] + nt_dot(jnp.concatenate(pairs, axis=0), w[p])

    weigh(0, w0, x0)

    def first(i, carry):
        weigh(2 * i + 1, w1, x1)
        multiply(2 * i, w0, x0)
        weigh(2 * i + 2, w0, x0)
        multiply(2 * i + 1, w1, x1)
        return carry

    lax.fori_loop(0, N_CH // 2 - 1, first, 0)
    late.start()
    for copy in table:
        copy.start()
    weigh(N_CH - 1, w1, x1)
    multiply(N_CH - 2, w0, x0)
    multiply(N_CH - 1, w1, x1)

    def fold3(rows):
        return rows[:, :256] + rows[:, 256:512] + rows[:, 512:]

    def group_sums(lanes):
        l = lax.broadcasted_iota(jnp.int32, (lanes, 128), 0)
        j = lax.broadcasted_iota(jnp.int32, (lanes, 128), 1)
        return jnp.where(l // CH == j, 1.0, 0.0).astype(F32)

    def diagonal(total):
        r = lax.broadcasted_iota(jnp.int32, total.shape, 0)
        l = lax.broadcasted_iota(jnp.int32, total.shape, 1)
        kept = jnp.where(r % CH == l % CH, total, 0.0)
        return jnp.sum(kept.reshape(total.shape[0] // CH, CH, total.shape[1]), axis=1)

    def pack(groups):
        ones = group_sums(groups)
        both = lax.dot_general(
            fold[:, :groups], ones, (((1,), (0,)), ((), ())),
            precision=lax.Precision.HIGHEST, preferred_element_type=F32,
        )
        upper = pltpu.roll(both[:8], 0, 1, stride=8, stride_axis=0)
        lower = pltpu.roll(both[8:], 64, 1, stride=8, stride_axis=0)
        return jnp.sum(upper + lower, axis=0, keepdims=True)

    def spread(slot, row, got, place, peers):
        pay[slot] = row
        got[slot, pl.ds(place, 1)] = row.reshape(1, 1, 128)
        for peer in peers:
            pltpu.make_async_remote_copy(
                src_ref=pay.at[slot],
                dst_ref=got.at[slot, place],
                send_sem=rsend_sem.at[slot],
                recv_sem=rrecv_sem.at[slot],
                device_id=peer,
                device_id_type=MESH,
            ).start()

    def gathered(slot, got, peers):
        sent = got.at[slot, 0 : len(peers)]
        pltpu.make_async_copy(sent, sent, rsend_sem.at[slot]).wait()
        pltpu.make_async_copy(sent, sent, rrecv_sem.at[slot]).wait()
        rows = got[slot].reshape(len(peers) + 1, 128)
        return jnp.sum(rows, axis=0, keepdims=True)

    def unpack(row):
        same = jnp.broadcast_to(row, (8, 128))
        out = same
        for i in range(1, 8):
            out = jnp.where(row128 == i, pltpu.roll(same, 128 - 8 * i, 1), out)
        return out

    def lanes_sum(row, start):
        lanes = lax.broadcasted_iota(jnp.int32, (1, 128), 1)
        kept = jnp.where((lanes >= start) & (lanes < start + 8), row, 0.0)
        return jnp.sum(kept, axis=1, keepdims=True)

    def flip(matrix):
        out = jnp.zeros((8, 128), F32)
        for j in range(8):
            row = jnp.broadcast_to(matrix[j : j + 1], (8, 128))
            column = jnp.sum(jnp.where(row128 == lane128, row, 0.0), axis=1, keepdims=True)
            out = jnp.where(lane128 == j, column, out)
        return out

    def solve(matrix, right):
        m = jnp.where(lane128 < 8, matrix, jnp.where(lane128 == 8, right, 0.0))
        for k in range(8):
            column = jnp.broadcast_to(m[:, k : k + 1], (8, 128))
            row = m[k : k + 1] / column[k : k + 1]
            m = jnp.where(row128 == k, row, m - column * row)
        answer = jnp.broadcast_to(m[:, 8:9], (8, 128))
        for j in range(8):
            cvec[j] = jnp.broadcast_to(answer[j : j + 1], (8, 128))

    fold[...] = jnp.zeros_like(fold)
    fold[0:9] = diagonal(acc[0]) + diagonal(acc[1])
    fold[9:10] = fold3(jnp.sum(sq[...], axis=0, keepdims=True))
    fold[10:11] = fold3(jnp.sum(weights[...], axis=0, keepdims=True))
    row = pack(256)
    pl.semaphore_wait(barrier, len(others_all))
    spread(0, row, gota, col * N_GRP + grp, others_all)

    def prepare(i, carry):
        rows = pl.ds(pl.multiple_of(i * SUB, SUB), SUB)
        inside = met[rows] > 0.0
        precond = jnp.where(inside, pre[rows], 0.0)
        for p in range(2):
            density = dn[p, rows]
            residual = src[p, rows] - resp[rows] * density
            base[p, rows] = jnp.where(inside, density, 0.0) + precond * residual
            for j in range(HIST):
                if j < HIST - 1:
                    drho = hd[j, p, rows].astype(F32)
                else:
                    drho = (density - db[p, rows]).astype(BF16).astype(F32)
                dres = (hr[j, p, rows] if j < HIST - 1 else hn[0, p, rows]).astype(F32)
                step[j, p, rows] = jnp.where(inside, drho, 0.0) + precond * dres
        return carry

    late.wait()
    lax.fori_loop(0, COLS // SUB, prepare, 0)
    for copy in table:
        copy.wait()
    row = gathered(0, gota, others_all)
    margin = unpack(row)
    margin = 0.5 * (margin + flip(margin))
    amat[...] = jnp.where(lane128 < 8, margin, 0.0)
    lanes8 = jnp.broadcast_to(pltpu.roll(row, 64, 1), (8, 128))
    right = jnp.sum(jnp.where(row128 == lane128, lanes8, 0.0), axis=1, keepdims=True)
    weight_total = lanes_sum(row, 80)
    norm0 = jnp.sqrt(lanes_sum(row, 72) / weight_total)
    solve(amat[...], right)

    def mix(t, h, new):
        def go(i, carry):
            local = pl.multiple_of(i * SUB, SUB)
            rows = pl.ds(pl.multiple_of(h * HALF + i * SUB, SUB), SUB)
            coefficient = []
            for j in range(HIST):
                lanes = jnp.concatenate([cvec[j]] * (NZ // 128), axis=1)
                coefficient.append(jnp.concatenate([lanes] * (SUB // 8), axis=0))
            values = []
            for p in range(2):
                mixed = base[p, rows]
                for j in range(HIST):
                    mixed = mixed - coefficient[j] * step[t + j, p, rows]
                new[p, rows] = mixed
                values.append(mixed * SCALE)
            re, im = values[0].astype(BF16), values[1].astype(BF16)
            rmat[h, 0, pl.ds(local, SUB)] = re
            rmat[h, 0, pl.ds(HALF + local, SUB)] = im
            rmat[h, 1, pl.ds(local, SUB)] = im
            rmat[h, 1, pl.ds(HALF + local, SUB)] = (-values[0]).astype(BF16)
            return carry

        lax.fori_loop(0, HALF // SUB, go, 0)

    def transform(t, h, low, high):
        planes = nt_dot(tab[low:high, :NZ], rmat[h, 0]) - nt_dot(tab[low:high, NZ:], rmat[h, 1])
        for p in range(2):
            part = planes[:, p * HALF : (p + 1) * HALF]
            if t == 0:
                prod[h, p, low:high] = part
            else:
                whole[p, low:high, h * HALF : (h + 1) * HALF] = part

    def out_block(t, h):
        start, size = (col * COLS, COLS) if h is None else (col * COLS + h * HALF, HALF)
        return slab_o.at[t, :, :, pl.ds(pl.multiple_of(start, HALF), size)]

    def block(h, dy, dz, dc):
        start = place[dy] * 8 * ZB + (zs[dz] + cs[dc]) * ZB
        planes = whole if h is None else prod.at[h]
        return planes.at[:, pl.ds(pl.multiple_of(start, 8), ZB)]

    def own(t, h):
        return pltpu.make_async_copy(block(h, 0, 0, 0), out_block(t, h), own_sem)

    def send(t, h, pairs):
        for dy, dz in pairs:
            for dc in (1, 0):
                if dy or dz or dc:
                    pltpu.make_async_remote_copy(
                        src_ref=block(h, dy, dz, dc),
                        dst_ref=out_block(t, h),
                        send_sem=send_sem.at[t],
                        recv_sem=recv_sem.at[t],
                        device_id=(ys[dy] + zs[dz] + cs[dc], grp),
                        device_id_type=MESH,
                    ).start()
                else:
                    own(t, h).start()

    def finish(t):
        for h in (0, 1) if t == 0 else (None,):
            own(t, h).wait()
        rows = (N_COL - 1) * COLS
        blocks = slab_o.at[t, :, :, 0:rows]
        pltpu.make_async_copy(blocks, blocks, send_sem.at[t]).wait()
        pltpu.make_async_copy(blocks, blocks, recv_sem.at[t]).wait()

    mix(0, 0, d1)
    transform(0, 0, 0, NZ // 2)
    send(0, 0, near)
    transform(0, 0, NZ // 2, NZ)
    send(0, 0, far[:3])
    mix(0, 1, d1)

    sq[...] = jnp.zeros_like(sq)

    def second(i, carry):
        rows = pl.ds(pl.multiple_of(i * SUB, SUB), SUB)
        metric = met[rows]
        r = resp[rows]
        for p in range(2):
            s = src[p, rows]
            residual = s - r * d1[p, rows]
            earlier = s - r * dn[p, rows]
            newest = (residual - earlier).astype(BF16)
            hn[1, p, rows] = newest
            sq[...] += metric * residual * residual
            half = residual.astype(BF16).astype(F32)
            w2[p, 0, rows] = (metric * newest.astype(F32)).astype(BF16)
            w2[p, 1, rows] = (metric * half).astype(BF16)
        return carry

    def products():
        totals = [jnp.zeros((8 * CH, 2 * CH), F32)] * 2
        for ch in range(N_CH):
            rows = slice(ch * CH, (ch + 1) * CH)
            for p in range(2):
                pairs = [hr[1:7, p, rows].reshape(6 * CH, NZ), hn[0, p, rows], hn[1, p, rows]]
                totals[p] = totals[p] + nt_dot(
                    jnp.concatenate(pairs, axis=0), w2[p, :, rows].reshape(2 * CH, NZ)
                )
        return diagonal(totals[0]) + diagonal(totals[1])

    lax.fori_loop(0, COLS // SUB, second, 0)
    total = products()
    fold[...] = jnp.zeros_like(fold)
    fold[0:8, 0 : 2 * CH] = total
    squares = fold3(jnp.sum(sq[...], axis=0, keepdims=True))
    fold[8:9, 0:128] = squares[:, :128] + squares[:, 128:]
    row = pack(128)
    spread(1, row, gota, col * N_GRP + grp, others_all)
    send(0, 0, far[3:])

    def renew(i, carry):
        rows = pl.ds(pl.multiple_of(i * SUB, SUB), SUB)
        inside = met[rows] > 0.0
        precond = jnp.where(inside, pre[rows], 0.0)
        for p in range(2):
            density = d1[p, rows]
            residual = src[p, rows] - resp[rows] * density
            base[p, rows] = jnp.where(inside, density, 0.0) + precond * residual
            drho = (density - dn[p, rows]).astype(BF16).astype(F32)
            dres = hn[1, p, rows].astype(F32)
            step[HIST, p, rows] = jnp.where(inside, drho, 0.0) + precond * dres
        return carry

    lax.fori_loop(0, COLS // SUB, renew, 0)
    transform(0, 1, 0, NZ)
    send(0, 1, near + far)
    row = gathered(1, gota, others_all)
    table1 = unpack(row)
    newest = table1[:, 0:1]
    across = jnp.sum(jnp.where(row128 == lane128, newest, 0.0), axis=0, keepdims=True)
    shifted = pltpu.roll(pltpu.roll(amat[...], 7, 0), 127, 1)
    matrix = jnp.where(lane128 == 7, newest, jnp.where(row128 == 7, across, shifted))
    norm1 = jnp.sqrt(lanes_sum(row, 64) / weight_total)
    solve(matrix, table1[:, 1:2])

    for h in range(2):
        mix(1, h, mix_o)
        transform(1, h, 0, NZ)
    send(1, None, last)
    lanes = lax.broadcasted_iota(jnp.int32, (1, 128), 1)
    norm_o[...] = jnp.where(lanes == 0, norm0, jnp.where(lanes == 1, norm1, 0.0))
    finish(0)
    finish(1)


def deliver(slab_v, mix_v, norm_v, slab_o, mix_o, norm_o, sem):
    copies = []
    for p in range(2):
        for t in range(ITERS):
            for z in range(0, ZB, 8):
                at = (t, p, pl.ds(z, 8))
                copies.append((slab_v.at[at], slab_o.at[at]))
        for k in range(0, COLS, COLS // 4):
            at = (p, pl.ds(k, COLS // 4))
            copies.append((mix_v.at[at], mix_o.at[at]))
    copies = [pltpu.make_async_copy(a, b, sem.at[i]) for i, (a, b) in enumerate(copies)]
    for copy in copies:
        copy.start()
    lanes = lax.broadcasted_iota(jnp.int32, (1, 128), 1)
    for t in range(ITERS):
        norm_o[t] = jnp.sum(jnp.where(lanes == t, norm_v[...], 0.0))
    for copy in copies:
        copy.wait()


def body(dn, db, src, resp, hd, hr, shell, screening):
    any_spec = pl.BlockSpec(memory_space=pl.ANY)
    hbm = pl.BlockSpec(memory_space=pltpu.HBM)
    smem = pl.BlockSpec(memory_space=pltpu.SMEM)
    stack = (2, COLS, NZ)
    vmem = pl.BlockSpec(memory_space=pltpu.VMEM)
    slab_shape = (ITERS, 2, ZB, N_COL * COLS)
    parts = pl.pallas_call(
        kernel,
        out_shape=(pltpu.VMEM(slab_shape, F32), pltpu.VMEM(stack, F32), pltpu.VMEM((1, 128), F32)),
        in_specs=[hbm] * 9,
        out_specs=(vmem, vmem, vmem),
        scratch_shapes=[
            pltpu.SMEM((COLS,), jnp.int32),
            pltpu.SMEM((1,), F32),
            pltpu.VMEM(stack, F32),
            pltpu.VMEM(stack, F32),
            pltpu.VMEM(stack, F32),
            pltpu.VMEM((COLS, NZ), F32),
            pltpu.VMEM((7,) + stack, BF16),
            pltpu.VMEM((7,) + stack, BF16),
            pltpu.VMEM((2,) + stack, BF16),
            pltpu.VMEM((NZ, 2 * NZ), BF16),
            pltpu.VMEM(stack, F32),
            pltpu.VMEM((COLS, NZ), F32),
            pltpu.VMEM((COLS, NZ), F32),
            pltpu.VMEM(stack, F32),
            pltpu.VMEM((9,) + stack, F32),
            pltpu.VMEM((2, HIST * CH, NZ), BF16),
            pltpu.VMEM((2, HIST * CH, NZ), BF16),
            pltpu.VMEM((2, 2 * CH, NZ), BF16),
            pltpu.VMEM((2, 2 * CH, NZ), BF16),
            pltpu.VMEM((2, 2, COLS, NZ), BF16),
            pltpu.VMEM((2, 9 * CH, HIST * CH), F32),
            pltpu.VMEM((SUB, NZ), F32),
            pltpu.VMEM((8, NZ), F32),
            pltpu.VMEM((16, 256), F32),
            pltpu.VMEM((8, 128), F32),
            pltpu.VMEM((8, 8, 128), F32),
            pltpu.VMEM((2, 2, COLS, NZ), BF16),
            pltpu.VMEM((2, 2, NZ, HALF), F32),
            pltpu.VMEM((2, NZ, COLS), F32),
            pltpu.VMEM((2, 1, 128), F32),
            pltpu.VMEM((2, N_COL * N_GRP, 1, 128), F32),
            pltpu.SemaphoreType.DMA((2,)),
            pltpu.SemaphoreType.DMA((N_CH,)),
            pltpu.SemaphoreType.DMA,
            pltpu.SemaphoreType.DMA((4,)),
            pltpu.SemaphoreType.DMA,
            pltpu.SemaphoreType.DMA((ITERS,)),
            pltpu.SemaphoreType.DMA((ITERS,)),
            pltpu.SemaphoreType.DMA((2,)),
            pltpu.SemaphoreType.DMA((2,)),
        ],
        compiler_params=pltpu.CompilerParams(
            collective_id=0, has_side_effects=True, vmem_limit_bytes=54 * 1024 * 1024
        ),
        name="mixing",
    )(dn, db, src, resp, hd, hr, shell, screening, plane_table())
    return pl.pallas_call(
        deliver,
        out_shape=(
            jax.ShapeDtypeStruct(slab_shape, F32),
            jax.ShapeDtypeStruct(stack, F32),
            jax.ShapeDtypeStruct((ITERS,), F32),
        ),
        in_specs=[vmem, vmem, vmem],
        out_specs=(any_spec, any_spec, smem),
        scratch_shapes=[pltpu.SemaphoreType.DMA((20,))],
        compiler_params=pltpu.CompilerParams(vmem_limit_bytes=16 * 1024 * 1024),
        name="deliver",
    )(*parts)


def solution(mesh):
    columns = ("col", "grp")
    return jax.shard_map(
        body,
        mesh=mesh,
        in_specs=(
            P(None, columns, None),
            P(None, columns, None),
            P(None, columns, None),
            P(columns, None),
            P(None, None, columns, None),
            P(None, None, columns, None),
            P(columns),
            P(),
        ),
        out_specs=(P(None, None, "col", "grp"), P(None, columns, None), P()),
        check_vma=False,
    )
```

time: 75.9 us -> 60.6 us (0.80)
  Pallas kernels: 74.5 us -> 59.2 us
    pallas_call x1, Pallas kernels: 71.8 us -> 56.3 us  [body(): pl.pallas_call(kernel, out_shape=(pltpu.VMEM(slab_shape, F32), pltpu.VMEM...]
where the time goes in v2:
time: 60.6 us; the launch traced here: 60.4 us
  Pallas kernels  59.2 us (98%)
  between operations  1.29 us (2%)
    pallas_call x1, Pallas kernels, body(): pl.pallas_call(kernel, out_shape=(pltpu.VMEM(slab_shape, F32), pltpu.VMEM...  56.3 us
    pallas_call x1, Pallas kernels, body(): pl.pallas_call(deliver, out_shape=(jax.ShapeDtypeStruct(slab_shape, F32),...  2.85 us

profile of v2, /device:TPU:1, one launch (start us, length us, event | category | flops | bytes accessed | tf_op | source)
XLA Modules:
  0.0 60.4 jit_solution(176711512344515205)
XLA Ops:
  1.3 56.3 %mixing.1 = (f32[2,2,24,8192]{3,2,1,0:T(8,128)S(1)}, f32[2,256,768]{2,1,0:T(8,128)S(1)}, f32[1,128]{1,0:T(1,128)S(1)}) custom-call(f32[2,256,768]{2,1,0:T(8,128)} %dn_h.1, f32[2,256,768]{2,1,0:T(8,128)} %db_h.1, f32[2,256,768]{2,1,0:T(8,128)} %src_h.1, f32[256,768]{1,0:T(8,128)} %resp_h.1, bf16[7,2,256,768]{3,2,1,0:T(8,128)(2,1)} %hd_h.1, ...), custom_call_target="tpu_custom_call" | custom-call | tf_op jit(solution)/shard_map/mixing/pallas_call | solution.py:459
  57.6 2.8 %deliver.1 = (f32[2,2,24,8192]{3,2,1,0:T(8,128)}, f32[2,256,768]{2,1,0:T(8,128)}, f32[2]{0:T(128)}) custom-call(f32[2,2,24,8192]{3,2,1,0:T(8,128)S(1)} %get-tuple-element.6.slab_v, f32[2,256,768]{2,1,0:T(8,128)S(1)} %get-tuple-element.7.mix_v, f32[1,128]{1,0:T(1,128)S(1)} %get-tuple-element.8.norm_v), custom_call_target="tpu_custom_call" | custom-call | tf_op jit(solution)/shard_map/deliver/pallas_call | solution.py:511

commit v3 on v2

--- a/solution.py
+++ b/solution.py
@@ -429,7 +429,7 @@
     finish(1)
 
 
-def deliver(slab_v, mix_v, norm_v, slab_o, mix_o, norm_o, sem):
+def deliver(slab_v, mix_v, norm_v, slab_o, mix_o, norm_o, norm_s, sem):
     copies = []
     for p in range(2):
         for t in range(ITERS):
@@ -444,15 +444,16 @@
         copy.start()
     lanes = lax.broadcasted_iota(jnp.int32, (1, 128), 1)
     for t in range(ITERS):
-        norm_o[t] = jnp.sum(jnp.where(lanes == t, norm_v[...], 0.0))
+        norm_s[t] = jnp.sum(jnp.where(lanes == t, norm_v[...], 0.0))
+    norms = pltpu.make_async_copy(norm_s, norm_o, sem.at[len(copies)])
+    norms.start()
     for copy in copies:
         copy.wait()
+    norms.wait()
 
 
 def body(dn, db, src, resp, hd, hr, shell, screening):
-    any_spec = pl.BlockSpec(memory_space=pl.ANY)
     hbm = pl.BlockSpec(memory_space=pltpu.HBM)
-    smem = pl.BlockSpec(memory_space=pltpu.SMEM)
     stack = (2, COLS, NZ)
     vmem = pl.BlockSpec(memory_space=pltpu.VMEM)
     slab_shape = (ITERS, 2, ZB, N_COL * COLS)
@@ -516,8 +517,8 @@
             jax.ShapeDtypeStruct((ITERS,), F32),
         ),
         in_specs=[vmem, vmem, vmem],
-        out_specs=(any_spec, any_spec, smem),
-        scratch_shapes=[pltpu.SemaphoreType.DMA((20,))],
+        out_specs=(hbm, hbm, hbm),
+        scratch_shapes=[pltpu.SMEM((ITERS,), F32), pltpu.SemaphoreType.DMA((21,))],
         compiler_params=pltpu.CompilerParams(vmem_limit_bytes=16 * 1024 * 1024),
         name="deliver",
     )(*parts)

time: 60.6 us -> 60.1 us (level)
  no operation moved by 1% of the time
where the time goes in v3:
time: 60.1 us; the launch traced here: 59.9 us
  Pallas kernels  58.7 us (98%)
  between operations  1.29 us (2%)
    pallas_call x1, Pallas kernels, body(): pl.pallas_call(kernel, out_shape=(pltpu.VMEM(slab_shape, F32), pltpu.VMEM...  56.3 us
    pallas_call x1, Pallas kernels, body(): pl.pallas_call(deliver, out_shape=(jax.ShapeDtypeStruct(slab_shape, F32),...  2.35 us

profile of v3, /device:TPU:1, one launch (start us, length us, event | category | flops | bytes accessed | tf_op | source)
XLA Modules:
  0.0 59.9 jit_solution(15212375580322445837)
XLA Ops:
  1.3 56.3 %mixing.1 = (f32[2,2,24,8192]{3,2,1,0:T(8,128)S(1)}, f32[2,256,768]{2,1,0:T(8,128)S(1)}, f32[1,128]{1,0:T(1,128)S(1)}) custom-call(f32[2,256,768]{2,1,0:T(8,128)} %dn_h.1, f32[2,256,768]{2,1,0:T(8,128)} %db_h.1, f32[2,256,768]{2,1,0:T(8,128)} %src_h.1, f32[256,768]{1,0:T(8,128)} %resp_h.1, bf16[7,2,256,768]{3,2,1,0:T(8,128)(2,1)} %hd_h.1, ...), custom_call_target="tpu_custom_call" | custom-call | tf_op jit(solution)/shard_map/mixing/pallas_call | solution.py:460
  57.6 2.4 %deliver.1 = (f32[2,2,24,8192]{3,2,1,0:T(8,128)}, f32[2,256,768]{2,1,0:T(8,128)}, f32[2]{0:T(128)}) custom-call(f32[2,2,24,8192]{3,2,1,0:T(8,128)S(1)} %get-tuple-element.6.slab_v, f32[2,256,768]{2,1,0:T(8,128)S(1)} %get-tuple-element.7.mix_v, f32[1,128]{1,0:T(1,128)S(1)} %get-tuple-element.8.norm_v), custom_call_target="tpu_custom_call" | custom-call | tf_op jit(solution)/shard_map/deliver/pallas_call | solution.py:512

commit v4 on v3

--- a/solution.py
+++ b/solution.py
@@ -60,11 +60,16 @@
         (2, 2), (2, 1), (2, 3), (1, 2), (3, 2), (2, 0), (0, 2), (1, 1),
         (3, 3), (1, 3), (3, 1), (0, 0), (1, 0), (3, 0), (0, 1), (0, 3),
     ]
-    others_all = [
-        (ys[dy] + zs[dz] + cs[dc], (grp + dx) % 4)
+    offsets = [
+        (dy, dz, dx, dc)
         for dy in (2, 1, 3, 0) for dz in (2, 1, 3, 0) for dx in (2, 1, 3, 0) for dc in (1, 0)
         if dx or dy or dz or dc
     ]
+    offsets.sort(key=lambda d: -sum(min(step, 4 - step) for step in d[:3]))
+    others_all = [
+        (ys[dy] + zs[dz] + cs[dc], (grp + dx) % 4) for dy, dz, dx, dc in offsets
+    ]
+
     def early(ch):
         rows = pl.ds(pl.multiple_of(ch * CH, CH), CH)
         return [

time: 60.1 us -> 59.9 us (level)
  no operation moved by 1% of the time
where the time goes in v4:
time: 59.9 us; the launch traced here: 59.8 us
  Pallas kernels  58.5 us (98%)
  between operations  1.29 us (2%)
    pallas_call x1, Pallas kernels, body(): pl.pallas_call(kernel, out_shape=(pltpu.VMEM(slab_shape, F32), pltpu.VMEM...  56.2 us
    pallas_call x1, Pallas kernels, body(): pl.pallas_call(deliver, out_shape=(jax.ShapeDtypeStruct(slab_shape, F32),...  2.35 us

profile of v4, /device:TPU:1, one launch (start us, length us, event | category | flops | bytes accessed | tf_op | source)
XLA Modules:
  0.0 59.8 jit_solution(8893225001663553341)
XLA Ops:
  1.3 56.2 %mixing.1 = (f32[2,2,24,8192]{3,2,1,0:T(8,128)S(1)}, f32[2,256,768]{2,1,0:T(8,128)S(1)}, f32[1,128]{1,0:T(1,128)S(1)}) custom-call(f32[2,256,768]{2,1,0:T(8,128)} %dn_h.1, f32[2,256,768]{2,1,0:T(8,128)} %db_h.1, f32[2,256,768]{2,1,0:T(8,128)} %src_h.1, f32[256,768]{1,0:T(8,128)} %resp_h.1, bf16[7,2,256,768]{3,2,1,0:T(8,128)(2,1)} %hd_h.1, ...), custom_call_target="tpu_custom_call" | custom-call | tf_op jit(solution)/shard_map/mixing/pallas_call | solution.py:465
  57.5 2.4 %deliver.1 = (f32[2,2,24,8192]{3,2,1,0:T(8,128)}, f32[2,256,768]{2,1,0:T(8,128)}, f32[2]{0:T(128)}) custom-call(f32[2,2,24,8192]{3,2,1,0:T(8,128)S(1)} %get-tuple-element.6.slab_v, f32[2,256,768]{2,1,0:T(8,128)S(1)} %get-tuple-element.7.mix_v, f32[1,128]{1,0:T(1,128)S(1)} %get-tuple-element.8.norm_v), custom_call_target="tpu_custom_call" | custom-call | tf_op jit(solution)/shard_map/deliver/pallas_call | solution.py:517
